TPU v7x, 32 devices: a whole 2x2x4 slice. The times are simulated.
32 devices in a mesh: seq: 4 (over y, x), exp: 8 (over z, core).
Axes of the slice: x: 2, y: 2, z: 4, core: 2. Of those that a mesh axis runs over, the one named last changes fastest.
Arguments:
- gates: float32 [4096, 2], P(('seq', 'exp')), may hold values from 0.1 to 0.9
- expert_ids: int32 [4096, 2], P(('seq', 'exp')), may hold values from 0 to 7, all different within a row; in each aligned block of 128 rows (0 to 127, 128 to 255, ...) at most 32 rows name the same one
- saved_pre: bfloat16 [8, 1024, 2, 7168], P('exp', None, None, 'seq'), may hold values from -6 to 6
- w_down: bfloat16 [8, 7168, 4096], P('exp', 'seq'), may hold values from -0.0625 to 0.0625
- residual_grad: bfloat16 [4096, 4096], P(('seq', 'exp')), may hold values from -6 to 6
- in_weight: bfloat16 [4096, 2048], P('seq', 'exp'), may hold values from -0.125 to 0.125
- ssm_in: bfloat16 [4096, 2048], P('seq', 'exp'), may hold values from -0.59765625 to 0.59765625
- b_proj: bfloat16 [4096, 128], P('seq'), may hold values from -0.546875 to 0.546875
- c_proj: bfloat16 [4096, 128], P('seq'), may hold values from -0.546875 to 0.546875
- step_sizes: float32 [32, 4096], P('exp', 'seq'), may hold values from 0.05 to 1149.88
- a_log: float32 [32], P('exp'), may hold values from -12 to 0
- skip_gain: float32 [32], P('exp'), may hold values from 0.5 to 1.5
- ssm_grad: bfloat16 [4096, 2048], P('seq', 'exp'), may hold values from -6 to 6
Outputs:
- pre_grads: bfloat16 [8, 1024, 2, 7168], P('exp', None, None, 'seq')
- route_grads: float32 [4096, 2], P(('seq', 'exp'))
- b_grads: float32 [4096, 128], P(('seq', 'exp'))
- c_grads: float32 [4096, 128], P(('seq', 'exp'))
- step_grads: float32 [32, 4096], P('exp', 'seq')
Inputs may be any that keep to these rules, and one draw needn't show every extreme that they name: `expert_ids`: in each aligned block of 128 rows every expert is named by exactly 32 entries, and a row names 2 different experts.
All inputs are finite; a program needn't handle non-finite values.
Results may differ from a plain program's by a relative error of at most 0.019.
Values may be sent and summed in bfloat16 or wider, within the bound.
A program may use at most 192 MiB of HBM per device.

v0:
```python
import jax
import jax.numpy as jnp
from jax import lax
from jax.sharding import PartitionSpec as P

TOPK = 2
HDIM = 64
SPAN = 256


PRECISE = lax.Precision.HIGHEST
F32 = jnp.float32
BF16 = jnp.bfloat16


def mm(spec, a, b):
    return jnp.einsum(spec, a.astype(BF16), b.astype(BF16), preferred_element_type=F32)


def slot_positions(flat_ids, expert_count):
    entries = flat_ids.shape[1]
    onehot = (flat_ids[:, :, None] == jnp.arange(expert_count, dtype=jnp.int32)).astype(BF16)
    lower = jnp.tril(jnp.ones((entries, entries), BF16))
    running = jnp.einsum("ij,bje->bie", lower, onehot, preferred_element_type=F32)
    return jnp.sum(onehot.astype(F32) * running, axis=2).astype(jnp.int32) - 1


def ssm_part(ssm_in, b_proj, c_proj, step_sizes, a_log, skip_gain, ssm_grad):
    length, columns = ssm_in.shape
    heads = columns // HDIM
    state = b_proj.shape[1]
    blocks = length // SPAN
    parts = lax.axis_size("seq")
    me = lax.axis_index("seq")
    x = ssm_in.reshape(blocks, SPAN, heads, HDIM).transpose(2, 0, 1, 3)
    g = ssm_grad.reshape(blocks, SPAN, heads, HDIM).transpose(2, 0, 1, 3)
    b = b_proj.reshape(blocks, SPAN, state)
    c = c_proj.reshape(blocks, SPAN, state)
    rates = jnp.exp(a_log)
    q = (step_sizes * rates[:, None]).reshape(heads, blocks, SPAN)
    upper = jnp.triu(jnp.ones((SPAN, SPAN), F32))
    cum = jnp.einsum("hkj,ji->hki", q, upper, precision=PRECISE)
    total = cum[:, :, -1]
    head_decay = jnp.exp(-cum)
    tail_decay = jnp.exp(cum - total[:, :, None])
    block_decay = jnp.exp(-total)
    fresh = mm("hkjp,kjn->hkpn", tail_decay[..., None] * x.astype(F32), b)
    back = mm("hkjp,kjn->hkpn", head_decay[..., None] * g.astype(F32), c)
    end_state = fresh[:, 0]
    for k in range(1, blocks):
        end_state = block_decay[:, k, None, None] * end_state + fresh[:, k]
    entry_grad = back[:, blocks - 1]
    for k in range(blocks - 2, -1, -1):
        entry_grad = block_decay[:, k, None, None] * entry_grad + back[:, k]
    shard_decay = jnp.exp(-jnp.sum(total, axis=1))
    packed = jnp.concatenate(
        [
            end_state,
            entry_grad,
            jnp.broadcast_to(shard_decay[:, None, None], (heads, 16, state)),
        ],
        axis=1,
    ).astype(BF16)
    everyone = lax.all_gather(packed, "seq", axis=0).astype(F32)

    lower_mask = jnp.tril(jnp.ones((SPAN, SPAN), jnp.bool_))
    spread = cum[:, :, :, None] - cum[:, :, None, :]
    weights = jnp.where(lower_mask, jnp.exp(-jnp.where(lower_mask, spread, 0.0)), 0.0)
    scores = mm("kin,kjn->kij", c, b)
    pair = mm("hkip,hkjp->hkij", g, x)
    mixed = weights * scores[None]
    cross = weights * pair
    products = mixed * pair
    row_sum = jnp.sum(products, axis=3)
    column_sum = jnp.sum(products, axis=2)
    x_within = mm("hkij,hkip->hkjp", mixed, g)
    cross_sum = jnp.sum(cross, axis=0)
    b_within = mm("kij,kin->kjn", cross_sum, c)
    c_within = mm("kij,kjn->kin", cross_sum, b)

    entry = jnp.zeros((heads, HDIM, state), F32)
    leave = jnp.zeros((heads, HDIM, state), F32)
    for i in range(parts - 1):
        decay = everyone[i][:, 2 * HDIM : 2 * HDIM + 1, :]
        entry = jnp.where(i < me, decay * entry + everyone[i][:, :HDIM], entry)
    for i in range(parts - 1, 0, -1):
        decay = everyone[i][:, 2 * HDIM : 2 * HDIM + 1, :]
        leave = jnp.where(i > me, decay * leave + everyone[i][:, HDIM : 2 * HDIM], leave)
    entries = [entry]
    for k in range(blocks - 1):
        entries.append(block_decay[:, k, None, None] * entries[-1] + fresh[:, k])
    leaves = [leave]
    for k in range(blocks - 1, 0, -1):
        leaves.append(block_decay[:, k, None, None] * leaves[-1] + back[:, k])
    entries = jnp.stack(entries, axis=1)
    leaves = jnp.stack(leaves[::-1], axis=1)

    from_leave = tail_decay[..., None] * mm("kjn,hkpn->hkjp", b, leaves)
    from_entry = head_decay[..., None] * mm("kin,hkpn->hkip", c, entries)
    x_grad = x_within + from_leave + skip_gain[:, None, None, None] * g.astype(F32)
    x_grad = x_grad.transpose(1, 2, 0, 3).reshape(length, columns).astype(BF16)
    b_grad = b_within + mm("hkjp,hkpn->kjn", tail_decay[..., None] * x.astype(F32), leaves)
    c_grad = c_within + mm("hkip,hkpn->kin", head_decay[..., None] * g.astype(F32), entries)
    carried = jnp.sum(g.astype(F32) * from_entry, axis=3)
    leaving = jnp.sum(x.astype(F32) * from_leave, axis=3)
    through = block_decay * jnp.sum(leaves * entries, axis=(2, 3))
    after = jnp.einsum("hki,ij->hkj", row_sum - column_sum + carried, jnp.tril(jnp.ones((SPAN, SPAN), F32)), precision=PRECISE)
    before = jnp.einsum("hkj,ji->hki", leaving, jnp.triu(jnp.ones((SPAN, SPAN), F32), 1), precision=PRECISE)
    decay_grad = -(after + before + through[:, :, None])
    step_grads = decay_grad.reshape(heads, length) * rates[:, None]
    return (x_grad, b_grad.reshape(length, state), c_grad.reshape(length, state), step_grads)


def swiglu_grads(upstream, gate_values, saved_rows):
    gate_pre = saved_rows[:, 0:1, :].astype(F32)
    up_pre = saved_rows[:, 1:2, :].astype(F32)
    sigmoid_gate = jax.nn.sigmoid(gate_pre)
    activated = gate_pre * sigmoid_gate
    up = upstream[:, None, :]
    route_part = jnp.sum(activated * up_pre * up, axis=(1, 2))
    hidden_grad = gate_values[:, None, None] * up
    gate_grad = hidden_grad * up_pre * sigmoid_gate * (1.0 + gate_pre * (1.0 - sigmoid_gate))
    up_grad = hidden_grad * activated
    first = lax.broadcasted_iota(jnp.int32, saved_rows.shape, 1) == 0
    return (jnp.where(first, gate_grad, up_grad).astype(BF16), route_part)


def per_device(
    gates,
    expert_ids,
    saved_pre,
    w_down,
    residual_grad,
    in_weight,
    ssm_in,
    b_proj,
    c_proj,
    step_sizes,
    a_log,
    skip_gain,
    ssm_grad,
):
    expert_count = lax.axis_size("exp")
    parts = lax.axis_size("seq")
    my_expert = lax.axis_index("exp")
    my_part = lax.axis_index("seq")
    tokens_here, width = residual_grad.shape
    per_block = tokens_here * TOPK
    capacity = per_block // expert_count
    slots = expert_count * capacity

    routing = lax.all_gather(
        jnp.concatenate([gates, expert_ids.astype(F32)], axis=1), "exp", axis=0
    )
    part_gates = routing[:, :, :TOPK].reshape(expert_count, per_block)
    part_ids = routing[:, :, TOPK:].astype(jnp.int32).reshape(expert_count, per_block)
    slice_weight = lax.all_gather(in_weight, "exp", axis=0)
    positions = slot_positions(part_ids, expert_count)
    mine = (part_ids == my_expert)[:, None, :] & (
        positions[:, None, :] == jnp.arange(capacity, dtype=jnp.int32)[None, :, None]
    )
    part_slot_gates = jnp.sum(jnp.where(mine, part_gates[:, None, :], 0.0), axis=2).reshape(-1)
    slot_gates = lax.all_gather(part_slot_gates, "seq", axis=0, tiled=True)
    part_targets = part_ids * capacity + positions
    hits = (
        part_targets.reshape(expert_count, 1, tokens_here, TOPK)
        == jnp.arange(slots, dtype=jnp.int32)[None, :, None, None]
    )
    selector = jnp.any(hits, axis=3).astype(BF16)
    own_selector = lax.dynamic_index_in_dim(selector, my_expert, 0, keepdims=False)
    outgoing = jnp.dot(own_selector, residual_grad, preferred_element_type=F32).astype(BF16)
    depth = width // parts
    outgoing = outgoing.reshape(slots, parts, depth).transpose(1, 0, 2)
    residual_rows = lax.all_to_all(
        outgoing.reshape(parts * expert_count, capacity, depth), ("seq", "exp"), 0, 0, tiled=True
    ).reshape(parts * slots, depth)

    x_grad, b_grad, c_grad, step_grads = ssm_part(
        ssm_in, b_proj, c_proj, step_sizes, a_log, skip_gain, ssm_grad
    )

    columns = x_grad.shape[1]
    picked = jnp.einsum(
        "bst,btc->bsc",
        selector,
        x_grad.reshape(expert_count, tokens_here, columns),
        preferred_element_type=F32,
    ).astype(BF16)
    picked = picked.reshape(expert_count, expert_count, capacity, columns).transpose(1, 0, 2, 3)
    rows = lax.all_to_all(
        picked.reshape(expert_count, slots, columns), "exp", 0, 0, tiled=True
    )
    rows = rows.transpose(1, 0, 2).reshape(slots, expert_count * columns)
    all_rows = lax.all_gather(rows, "seq", axis=0, tiled=True)
    wide = slice_weight.transpose(1, 0, 2).reshape(depth, expert_count * columns)
    summed = lax.dot_general(all_rows, wide, (((1,), (1,)), ((), ())), preferred_element_type=F32)
    moe_rows = (residual_rows.astype(F32) + summed).astype(BF16)
    gathered = lax.all_gather(moe_rows, "seq", axis=0)

    both, gathered = lax.optimization_barrier(
        (jnp.concatenate([b_grad, c_grad], axis=1), gathered)
    )
    both = lax.psum_scatter(both, "exp", scatter_dimension=0, tiled=True)
    state = b_proj.shape[1]

    upstream = sum(
        lax.dot_general(
            gathered[i],
            w_down[0][:, i * depth : (i + 1) * depth],
            (((1,), (1,)), ((), ())),
            preferred_element_type=F32,
        )
        for i in range(parts)
    )
    pre_grad, route_part = swiglu_grads(upstream, slot_gates, saved_pre[0])
    everyone = lax.all_gather(route_part, "seq", axis=0)
    own = lax.dynamic_slice_in_dim(everyone, my_part * slots, slots, 1)
    own = jnp.sum(own, axis=0).reshape(expert_count, capacity)
    totals = lax.all_to_all(own, "exp", 0, 0, tiled=True).reshape(-1)
    own_target = lax.dynamic_index_in_dim(part_targets, my_expert, 0, keepdims=False)
    chosen = own_target[:, None] == jnp.arange(slots, dtype=jnp.int32)[None, :]
    route_grads = jnp.sum(jnp.where(chosen, totals[None, :], 0.0), axis=1)
    return (
        pre_grad[None],
        route_grads.reshape(tokens_here, TOPK),
        both[:, :state],
        both[:, state:],
        step_grads,
    )


def solution(mesh):
    in_specs = (
        P(("seq", "exp"), None),
        P(("seq", "exp"), None),
        P("exp", None, None, "seq"),
        P("exp", "seq", None),
        P(("seq", "exp"), None),
        P("seq", "exp"),
        P("seq", "exp"),
        P("seq", None),
        P("seq", None),
        P("exp", "seq"),
        P("exp"),
        P("exp"),
        P("seq", "exp"),
    )
    out_specs = (
        P("exp", None, None, "seq"),
        P(("seq", "exp"), None),
        P(("seq", "exp"), None),
        P(("seq", "exp"), None),
        P("exp", "seq"),
    )
    return jax.shard_map(
        per_device, mesh=mesh, in_specs=in_specs, out_specs=out_specs, check_vma=False
    )
```

profile of v0, /device:TPU:7, one launch (start us, length us, event | category | flops | bytes accessed | tf_op | source)
XLA Modules:
  0.0 342.2 jit_solution(9517445588619880855)
XLA Ops:
  7.3 0.7 all-gather.11.cloned.1.call-update
  8.0 0.7 exp.31
  8.7 0.7 convert_element_type.109
  9.4 0.7 pad_maximum_fusion.4
  10.1 13.5 %all-gather = f32[1024,4]{0,1:T(4,128)S(1)} all-gather(f32[128,4]{0,1:T(4,128)S(1)} %pad_maximum_fusion.4), channel_id=2, replica_groups=mesh['seq'=4,'exp'=8] {'exp'}, dimensions={0}, use_global_device_ids=true | all-gather | bytes 18432 | tf_op jit(solution)/shard_map/all_gather | solution.py:152
  23.6 0.8 broadcast_multiply_fusion.1
  25.0 0.6 fusion.136
  26.5 0.6 copy.165
  27.1 1.2 copy.154
  28.4 1.2 reshape.206
  30.0 0.5 copy.157
  30.8 1.3 convolution_bitcast_fusion.3
  32.7 8.7 %all_gather.37 = bf16[4,4,144,128]{3,2,1,0:T(8,128)(2,1)S(1)} all-gather(bf16[1,4,144,128]{3,2,1,0:T(8,128)(2,1)S(1)} %pad_maximum_fusion.3), channel_id=1, replica_groups=mesh['seq'=4,'exp'=8] {'seq'}, dimensions={0}, use_global_device_ids=true | all-gather | bytes 737280 | tf_op jit(solution)/shard_map/all_gather | solution.py:64
  41.9 0.6 slice_multiply_fusion
  43.3 0.9 fusion.60
  44.3 2.2 fusion.50
  46.6 2.3 copy.192
  48.8 2.8 reshape.237
  51.6 0.9 fusion.37
  52.5 1.6 convolution_convert_fusion.1
  54.2 30.4 %all_to_all.19 = bf16[8,256,256]{2,1,0:T(8,128)(2,1)} all-to-all(bf16[8,256,256]{2,1,0:T(8,128)(2,1)S(1)} %bitcast.292), channel_id=1, replica_groups=mesh['seq'=4,'exp'=8] {'exp'}, dimensions={0} | all-to-all | bytes 2097152 | tf_op jit(solution)/shard_map/all_to_all | solution.py:190
  84.6 2.3 copy.173
  86.9 1.5 convolution_convert_fusion
  88.3 1.6 copy.222
  89.9 5.2 %all-to-all-start = ((bf16[32,32,1024]{2,1,0:T(8,128)(2,1)}), bf16[32,32,1024]{2,1,0:T(8,128)(2,1)}, u32[]{:S(2)}, u32[]{:S(2)}) async-start(bf16[32,32,1024]{2,1,0:T(8,128)(2,1)} %bitcast.284), calls=%async_computation | async-start | bytes 4194304 | tf_op jit(solution)/shard_map/all_to_all | solution.py:174
  95.3 6.5 %copy.174 = bf16[1024,8,256]{0,2,1:T(8,128)(2,1)} copy(bf16[1024,8,256]{2,0,1:T(8,128)(2,1)} %bitcast.289) | data formatting | bytes 8388608 | tf_op jit(solution)/shard_map/transpose | solution.py:195
  101.8 41.7 %all-to-all-done = bf16[32,32,1024]{2,1,0:T(8,128)(2,1)} async-done(((bf16[32,32,1024]{2,1,0:T(8,128)(2,1)}), bf16[32,32,1024]{2,1,0:T(8,128)(2,1)}, u32[]{:S(2)}, u32[]{:S(2)}) %all-to-all-start) | async-done | bytes 2097184 | tf_op jit(solution)/shard_map/all_to_all | solution.py:174
  143.5 16.4 %all-gather.9.cloned.1.call-done = bf16[1024,2048]{0,1:T(8,128)(2,1)} async-done(((bf16[256,2048]{0,1:T(8,128)(2,1)}), bf16[1024,2048]{0,1:T(8,128)(2,1)}) %all-gather.9.cloned.1.call-update) | async-done | bytes 4194320 | tf_op jit(solution)/shard_map/all_gather | solution.py:194
  160.0 10.1 %fusion.10 = bf16[1024,1024]{1,0:T(8,128)(2,1)} fusion(bf16[32,32,1024]{2,1,0:T(8,128)(2,1)} %all-to-all-done, bf16[1024,2048]{0,1:T(8,128)(2,1)} %all-gather.9.cloned.1.call-done, bf16[1024,2048]{0,1:T(8,128)(2,1)} %bitcast.290), kind=kOutput, calls=%fused_computation.21 | convolution fusion | flops 4298113024 | bytes 12582912 | tf_op jit(solution)/shard_map/dot_general | solution.py:196
  170.1 1.3 copy.190
  171.4 1.6 copy.152
  173.0 1.6 copy.153
  174.6 0.6 broadcast_compare_fusion
  175.2 0.8 copy.150
  176.0 0.9 select_reduce_fusion.1
  176.9 0.6 reshape.225
  177.5 1.2 fusion.117
  178.8 0.8 add_bitcast_fusion
  179.6 1.3 multiply_reduce_fusion.1
  181.1 0.9 multiply_reduce_fusion.2
  181.9 1.6 fusion.53
  183.6 3.6 %fusion.21 = (f32[4,4,256]{2,1,0:T(4,128)S(1)}, f32[4,4,256]{2,1,0:T(4,128)S(1)}, bf16[4,256,256]{2,1,0:T(8,128)(2,1)S(1)}) fusion(f32[4,256,256]{2,1,0:T(8,128)S(1)} %copy-done.20, f32[4,4,256]{2,1,0:T(4,128)} %copy-done.26, pred[256,256]{1,0:T(8,128)(4,1)} %copy-done.29, bf16[4,256,4,64]{1,3,0,2:T(8,128)(2,1)} %copy.190, ...), kind=kOutput, calls=%fused_computation.34 | convolution fusion | flops 144433152 | bytes 2736128 | tf_op jit(solution)/shard_map/hkip,hkjp->hkij/dot_general | solution.py:17
  187.8 0.6 copy.198
  188.4 4.0 %copy.221 = bf16[1,1024,2,1792]{3,1,2,0:T(8,128)(2,1)} copy(bf16[1,1024,2,1792]{3,2,1,0:T(2,128)(2,1)S(1)} %bitcast.287) | data formatting | bytes 14680064 | tf_op args[2]
  192.4 7.5 %all-gather.4 = f32[4,1,256]{2,1,0:T(1,128)} all-gather(f32[1,1,256]{2,1,0:T(1,128)S(1)} %copy-done.41), channel_id=1, replica_groups=mesh['seq'=4,'exp'=8] {'seq'}, dimensions={0}, use_global_device_ids=true | all-gather | bytes 5120 | tf_op jit(solution)/shard_map/all_gather | solution.py:163
  199.9 0.5 iota_compare_fusion.10
  200.4 1.3 dynamic-slice_add_fusion
  202.0 1.4 convolution_bitcast_fusion.1
  204.1 1.0 pad_maximum_fusion
  205.1 0.7 broadcast_multiply_fusion
  205.8 50.7 %all-gather.13.cloned.1.call-done = bf16[4096,1024]{1,0:T(8,128)(2,1)} async-done(((bf16[1024,1024]{1,0:T(8,128)(2,1)}), bf16[4096,1024]{1,0:T(8,128)(2,1)}) %all-gather.13.cloned.1.call-update) | async-done | bytes 8388624 | tf_op jit(solution)/shard_map/all_gather | solution.py:198
  256.6 10.4 %fusion.15 = f32[1024,1792]{1,0:T(8,128)} fusion(bf16[1792,4096]{1,0:T(8,128)(2,1)} %bitcast.334, bf16[4,1024,1024]{2,1,0:T(8,128)(2,1)} %bitcast.340), kind=kOutput, calls=%fused_computation.28 | convolution fusion | flops 3758096384 | bytes 13107200 | tf_op jit(solution)/shard_map/dot_general | solution.py:207
  267.0 0.7 copy-done.45
  267.6 6.1 %fusion.17 = f32[1024,1792]{1,0:T(8,128)} fusion(bf16[1792,4096]{1,0:T(8,128)(2,1)S(1)} %bitcast.338, bf16[4,1024,1024]{2,1,0:T(8,128)(2,1)S(1)} %bitcast.342), kind=kOutput, calls=%fused_computation.30 | convolution fusion | flops 3758096384 | bytes 13107200 | tf_op jit(solution)/shard_map/dot_general | solution.py:207
  273.7 6.0 %fusion.19 = f32[1024,1792]{1,0:T(8,128)} fusion(bf16[1792,4096]{1,0:T(8,128)(2,1)S(1)} %bitcast.339, bf16[4,1024,1024]{2,1,0:T(8,128)(2,1)S(1)} %bitcast.343), kind=kOutput, calls=%fused_computation.32 | convolution fusion | flops 3758096384 | bytes 13107200 | tf_op jit(solution)/shard_map/dot_general | solution.py:207
  279.8 16.1 %fusion.4 = (f32[1024]{0:T(1024)S(1)}, f32[1024,1792]{1,0:T(8,128)}) fusion(bf16[1024,2,1792]{2,0,1:T(8,128)(2,1)} %bitcast.282, bf16[1792,4096]{1,0:T(8,128)(2,1)} %bitcast.335, bf16[4,1024,1024]{2,1,0:T(8,128)(2,1)} %bitcast.341, f32[1024,1792]{1,0:T(8,128)} %fusion.15, f32[1024,1792]{1,0:T(8,128)} %fusion.19, f32[1024,1792]{1,0:T(8,128)} %fusion.17), kind=kOutput, calls=%fused_computation.10 | convolution fusion | flops 3780115456 | bytes 42471424 | tf_op jit(solution)/shard_map/dot_general | solution.py:207
  295.9 6.5 %all-gather.3 = f32[4096]{0:T(1024)S(1)} all-gather(f32[1024]{0:T(1024)S(1)} %get-tuple-element.64), channel_id=5, replica_groups=mesh['seq'=4,'exp'=8] {'seq'}, dimensions={0}, use_global_device_ids=true | all-gather | bytes 20480 | tf_op jit(solution)/shard_map/all_gather | solution.py:216
  302.4 0.7 all_to_all.14
  303.1 7.2 %all-to-all-start.2 = ((f32[8,1,32]{2,1,0:T(1,128)}), f32[8,1,32]{2,1,0:T(1,128)S(1)}, u32[]{:S(2)}, u32[]{:S(2)}) async-start(f32[8,1,32]{2,1,0:T(1,128)} %all_to_all.14), calls=%async_computation.2 | async-start | bytes 8192 | tf_op jit(solution)/shard_map/all_to_all | solution.py:219
  310.3 8.6 %fusion.2 = (bf16[1024,1792]{1,0:T(8,128)(2,1)S(1)}, bf16[1024,1792]{1,0:T(8,128)(2,1)}) fusion(f32[1024,1792]{1,0:T(8,128)} %get-tuple-element.65, f32[1024]{0:T(1024)S(1)} %bitcast.329, bf16[1024,2,1792]{2,0,1:T(8,128)(2,1)} %bitcast.283), kind=kLoop, calls=%fused_computation.8 | loop fusion | flops 29360128 | bytes 22024192 | tf_op jit(solution)/shard_map/jit(_where)/broadcast_in_dim | solution.py:125
  318.9 13.1 %select_convert_fusion = bf16[1,1024,2,1792]{3,2,1,0:T(2,128)(2,1)} fusion(pred[2]{0:T(512)(128)(4,1)S(1)} %copy-done.44, bf16[1024,1792]{1,0:T(8,128)(2,1)} %get-tuple-element.51, bf16[1024,1792]{1,0:T(8,128)(2,1)S(1)} %get-tuple-element.50), kind=kLoop, calls=%fused_computation | loop fusion | flops 3670016 | bytes 14680066 | tf_op jit(solution)/shard_map/convert_element_type | solution.py:125
  332.5 0.7 reduce.16
  333.5 0.6 copy.181
  334.2 1.5 fusion.135
  (162 shorter events, 6.9 us)
Async XLA Ops:
  7.2 79.7 %copy-start = (bf16[128,4096]{1,0:T(8,128)(2,1)S(1)}, bf16[128,4096]{1,0:T(8,128)(2,1)}, u32[]{:S(2)}) copy-start(bf16[128,4096]{1,0:T(8,128)(2,1)} %param.17) | copy-start | bytes 3145732
  7.2 22.4 %copy-start.22 = (bf16[1024,256]{1,0:T(8,128)(2,1)S(1)}, bf16[1024,256]{1,0:T(8,128)(2,1)}, u32[]{:S(2)}) copy-start(bf16[1024,256]{1,0:T(8,128)(2,1)} %param.19) | copy-start | bytes 1572868
  7.2 23.6 %copy-start.3 = (bf16[1024,128]{1,0:T(8,128)(2,1)S(1)}, bf16[1024,128]{1,0:T(8,128)(2,1)}, u32[]{:S(2)}) copy-start(bf16[1024,128]{1,0:T(8,128)(2,1)} %param.21) | copy-start | bytes 786436
  7.2 24.9 %copy-start.2 = (bf16[1024,128]{1,0:T(8,128)(2,1)S(1)}, bf16[1024,128]{1,0:T(8,128)(2,1)}, u32[]{:S(2)}) copy-start(bf16[1024,128]{1,0:T(8,128)(2,1)} %param.20) | copy-start | bytes 786436
  7.2 88.1 %all-gather.11.cloned.1.call-start = ((), (), s32[]{:S(2)}) async-start(), calls=%async_computation.6 | async-start | bytes 4718592 | tf_op jit(solution)/shard_map/all_gather | solution.py:157
  7.9 152.0 %all-gather.9.cloned.1.call-start = ((), (), s32[]{:S(2)}) async-start(), calls=%async_computation.4 | async-start | bytes 5242880 | tf_op jit(solution)/shard_map/all_gather | solution.py:194
  8.7 14.9 %copy-start.42 = (f32[4]{0:T(128)}, f32[4]{0:T(128)S(1)}, u32[]{:S(2)}) copy-start(f32[4]{0:T(128)S(1)} %exp.31) | copy-start | bytes 52
  24.7 17.0 %copy-start.26 = (f32[4,4,256]{2,1,0:T(4,128)}, f32[4,4,256]{2,1,0:T(4,128)S(1)}, u32[]{:S(2)}) copy-start(f32[4,4,256]{2,1,0:T(4,128)S(1)} %fusion.77) | copy-start | bytes 49156
  25.0 7.4 %copy-start.31 = (f32[4,4,256]{2,0,1:T(4,128)}, f32[4,4,256]{2,0,1:T(4,128)S(1)}, u32[]{:S(2)}) copy-start(f32[4,4,256]{2,0,1:T(4,128)S(1)} %copy.162) | copy-start | bytes 49156
  25.8 6.3 %copy-start.9 = (s32[8,128,2]{0,2,1:T(2,128)}, s32[8,128,2]{0,2,1:T(2,128)S(1)}, u32[]{:S(2)}) copy-start(s32[8,128,2]{0,2,1:T(2,128)S(1)} %copy.149) | copy-start | bytes 24580
  25.9 0.6 copy-start.36
  26.1 6.5 %copy-start.28 = (s32[8,256]{1,0:T(8,128)}, s32[8,256]{1,0:T(8,128)S(1)}, u32[]{:S(2)}) copy-start(s32[8,256]{1,0:T(8,128)S(1)} %convert_add_fusion.1) | copy-start | bytes 24580
  30.7 10.9 %copy-start.37 = (f32[4]{0:T(128)}, f32[4]{0:T(128)S(1)}, u32[]{:S(2)}) copy-start(f32[4]{0:T(128)S(1)} %get-tuple-element.40) | copy-start | bytes 52
  30.7 11.7 %copy-start.38 = (f32[4]{0:T(128)}, f32[4]{0:T(128)S(1)}, u32[]{:S(2)}) copy-start(f32[4]{0:T(128)S(1)} %get-tuple-element.41) | copy-start | bytes 52
  30.7 11.7 %copy-start.39 = (f32[4]{0:T(128)}, f32[4]{0:T(128)S(1)}, u32[]{:S(2)}) copy-start(f32[4]{0:T(128)S(1)} %get-tuple-element.42) | copy-start | bytes 52
  32.4 10.2 %copy-start.4 = (bf16[1024,128]{1,0:T(8,128)(2,1)S(1)}, bf16[1024,128]{1,0:T(8,128)(2,1)}, u32[]{:S(2)}) copy-start(bf16[1024,128]{1,0:T(8,128)(2,1)} %param.21) | copy-start | bytes 786436
  41.5 2.8 copy-start.6
  41.5 2.8 copy-start.46
  41.6 0.8 copy-start.21
  41.6 2.6 copy-start.17
  41.6 2.6 copy-start.18
  41.7 2.6 copy-start.32
  41.7 2.6 copy-start.33
  41.7 2.5 copy-start.29
  41.8 2.5 copy-start.27
  42.6 1.7 copy-start.13
  42.6 1.7 copy-start.15
  42.7 0.7 copy-start.11
  43.0 1.3 copy-start.19
  52.5 1.6 copy-start.8
  89.9 53.6 %all-to-all-start = ((bf16[32,32,1024]{2,1,0:T(8,128)(2,1)}), bf16[32,32,1024]{2,1,0:T(8,128)(2,1)}, u32[]{:S(2)}, u32[]{:S(2)}) async-start(bf16[32,32,1024]{2,1,0:T(8,128)(2,1)} %bitcast.284), calls=%async_computation | async-start | bytes 4194304 | tf_op jit(solution)/shard_map/all_to_all | solution.py:174
  95.1 161.5 %all-gather.13.cloned.1.call-start = ((), (), s32[]{:S(2)}) async-start(), calls=%async_computation.7 | async-start | bytes 10485760 | tf_op jit(solution)/shard_map/all_gather | solution.py:198
  160.0 14.6 %copy-start.10 = (s32[8,128,2]{0,2,1:T(2,128)S(1)}, s32[8,128,2]{0,2,1:T(2,128)}, u32[]{:S(2)}) copy-start(s32[8,128,2]{0,2,1:T(2,128)} %copy-done.9) | copy-start | bytes 24580
  170.0 9.6 %copy-start.12 = (f32[4,1,64,128]{3,2,0,1:T(8,128)S(1)}, f32[4,1,64,128]{3,2,0,1:T(8,128)}, u32[]{:S(2)}) copy-start(f32[4,1,64,128]{3,2,0,1:T(8,128)} %copy-done.11) | copy-start | bytes 393220
  170.0 11.9 %copy-start.5 = (bf16[1024,128]{1,0:T(8,128)(2,1)S(1)}, bf16[1024,128]{1,0:T(8,128)(2,1)}, u32[]{:S(2)}) copy-start(bf16[1024,128]{1,0:T(8,128)(2,1)} %param.21) | copy-start | bytes 786436
  170.0 11.9 %copy-start.7 = (bf16[4,256,4,64]{1,0,3,2:T(4,128)(2,1)S(1)}, bf16[4,256,4,64]{1,0,3,2:T(4,128)(2,1)}, u32[]{:S(2)}) copy-start(bf16[4,256,4,64]{1,0,3,2:T(4,128)(2,1)} %reshape.206) | copy-start | bytes 1572868
  170.1 164.1 %reduce-scatter.2.cloned.1.call-start = ((), (), s32[]{:S(2)}) async-start(), calls=%async_computation.5 | async-start | bytes 1179648 | tf_op jit(solution)/shard_map/reduce_scatter | solution.py:203
  171.4 12.1 %copy-start.20 = (f32[4,256,256]{2,1,0:T(8,128)S(1)}, f32[4,256,256]{2,1,0:T(8,128)}, u32[]{:S(2)}) copy-start(f32[4,256,256]{2,1,0:T(8,128)} %copy-done.19) | copy-start | bytes 3145732
  178.8 0.8 copy-start.23
  179.6 1.3 copy-start.24
  179.6 1.3 copy-start.25
  181.9 6.4 %slice-start = ((s8[7340032]{0:T(1024)(128)(4,1)}), s8[4194304]{0:T(1024)(128)(4,1)S(1)}, s32[]{:S(2)}) async-start(s8[7340032]{0:T(1024)(128)(4,1)} %bitcast.286), calls=%async_computation.8 | async-start | bytes 8388608
  183.6 3.9 %copy-start.34 = (f32[4,4,256]{2,0,1:T(4,128)S(1)}, f32[4,4,256]{2,0,1:T(4,128)}, u32[]{:S(2)}) copy-start(f32[4,4,256]{2,0,1:T(4,128)} %get-tuple-element.66) | copy-start | bytes 49156
  183.6 4.8 %slice-start.1 = ((s8[7340032]{0:T(1024)(128)(4,1)}), s8[3145728]{0:T(1024)(128)(4,1)S(1)}, s32[]{:S(2)}) async-start(s8[7340032]{0:T(1024)(128)(4,1)} %bitcast.286), calls=%async_computation.9 | async-start | bytes 6291456
  188.4 4.0 %copy-start.41 = (f32[1,1,256]{2,1,0:T(1,128)S(1)}, f32[1,1,256]{2,1,0:T(1,128)}, u32[]{:S(2)}) copy-start(f32[1,1,256]{2,1,0:T(1,128)} %reshape.225) | copy-start | bytes 3076
  188.4 13.3 %copy-start.14 = (f32[4,1,64,128]{3,2,0,1:T(8,128)S(1)}, f32[4,1,64,128]{3,2,0,1:T(8,128)}, u32[]{:S(2)}) copy-start(f32[4,1,64,128]{3,2,0,1:T(8,128)} %copy-done.13) | copy-start | bytes 393220
  188.4 13.3 %copy-start.16 = (f32[4,64,128]{2,1,0:T(8,128)S(1)}, f32[4,64,128]{2,1,0:T(8,128)}, u32[]{:S(2)}) copy-start(f32[4,64,128]{2,1,0:T(8,128)} %copy-done.15) | copy-start | bytes 393220
  202.0 3.1 copy-start.30
  202.0 3.1 copy-start.43
  204.1 62.8 %slice-start.2 = ((s8[14680064]{0:T(1024)(128)(4,1)}), s8[2097152]{0:T(1024)(128)(4,1)S(1)}, s32[]{:S(2)}) async-start(s8[14680064]{0:T(1024)(128)(4,1)} %bitcast.336), calls=%async_computation.10 | async-start | bytes 4194304
  256.6 10.4 %slice-start.3 = ((s8[14680064]{0:T(1024)(128)(4,1)}), s8[4194304]{0:T(1024)(128)(4,1)S(1)}, s32[]{:S(2)}) async-start(s8[14680064]{0:T(1024)(128)(4,1)} %bitcast.336), calls=%async_computation.11 | async-start | bytes 8388608
  256.6 10.4 %slice-start.4 = ((s8[14680064]{0:T(1024)(128)(4,1)}), s8[4194304]{0:T(1024)(128)(4,1)S(1)}, s32[]{:S(2)}) async-start(s8[14680064]{0:T(1024)(128)(4,1)} %bitcast.336), calls=%async_computation.12 | async-start | bytes 8388608
  256.6 10.4 %slice-start.5 = ((s8[14680064]{0:T(1024)(128)(4,1)}), s8[4194304]{0:T(1024)(128)(4,1)S(1)}, s32[]{:S(2)}) async-start(s8[14680064]{0:T(1024)(128)(4,1)} %bitcast.336), calls=%async_computation.13 | async-start | bytes 8388608
  256.6 11.1 %copy-start.45 = (bf16[4096,1024]{1,0:T(8,128)(2,1)S(1)}, bf16[4096,1024]{1,0:T(8,128)(2,1)}, u32[]{:S(2)}) copy-start(bf16[4096,1024]{1,0:T(8,128)(2,1)} %all-gather.13.cloned.1.call-done) | copy-start | bytes 25165828
  279.8 30.5 %copy-start.35 = (f32[4,1,256]{2,1,0:T(1,128)S(1)}, f32[4,1,256]{2,1,0:T(1,128)}, u32[]{:S(2)}) copy-start(f32[4,1,256]{2,1,0:T(1,128)} %all-gather.4) | copy-start | bytes 12292
  303.1 28.9 %all-to-all-start.2 = ((f32[8,1,32]{2,1,0:T(1,128)}), f32[8,1,32]{2,1,0:T(1,128)S(1)}, u32[]{:S(2)}, u32[]{:S(2)}) async-start(f32[8,1,32]{2,1,0:T(1,128)} %all_to_all.14), calls=%async_computation.2 | async-start | bytes 8192 | tf_op jit(solution)/shard_map/all_to_all | solution.py:219
  310.3 8.6 %copy-start.44 = (pred[2]{0:T(512)(128)(4,1)S(1)}, pred[2]{0:T(512)(128)(4,1)}, u32[]{:S(2)}) copy-start(pred[2]{0:T(512)(128)(4,1)} %iota_compare_fusion.10) | copy-start | bytes 10
  318.9 16.8 %copy-start.1 = (bf16[128,4096]{1,0:T(8,128)(2,1)S(1)}, bf16[128,4096]{1,0:T(8,128)(2,1)}, u32[]{:S(2)}) copy-start(bf16[128,4096]{1,0:T(8,128)(2,1)} %param.17) | copy-start | bytes 3145732
  318.9 14.3 %copy-start.40 = (s32[1,256]{1,0:T(1,128)S(1)}, s32[1,256]{1,0:T(1,128)}, u32[]{:S(2)}) copy-start(s32[1,256]{1,0:T(1,128)} %dynamic-slice_add_fusion) | copy-start | bytes 3076
Sparse Core Ops, SparseCore 0:
  9.6 48.4 all-gather.10
  87.0 72.9 all-gather.8
  170.2 86.3 all-gather.12
  279.9 30.6 reduce-scatter.1
where the time goes:
time: 345 us; the launch traced here: 342 us
  waiting for transfers between devices  110 us (32%)
  blocking collectives  66.5 us (19%)
  matrix products  65.4 us (19%)
  other arithmetic  36.8 us (11%)
  local copies, waits for them, and re-layouts  36.5 us (11%)
  between operations  14.7 us (4%)
  starting transfers between devices  12.7 us (4%)
    all_gather x1, waiting for transfers between devices, per_device(): gathered = lax.all_gather(moe_rows, 'seq', axis=0)  50.7 us
    all_to_all x1, waiting for transfers between devices, per_device(): lax.all_to_all(outgoing.reshape(parts * expert_count, capacity, depth), (...  41.7 us
    dot_general x4, matrix products, per_device(): lax.dot_general(gathered[i], w_down[0][:, i * depth:(i + 1) * depth], (((...  38.6 us
    all_to_all x1, blocking collectives, per_device(): lax.all_to_all(picked.reshape(expert_count, slots, columns), 'exp', 0, 0,...  30.4 us
    all_gather x1, waiting for transfers between devices, per_device(): all_rows = lax.all_gather(rows, 'seq', axis=0, tiled=True)  16.4 us
    all_gather x1, blocking collectives, per_device(): lax.all_gather(jnp.concatenate([gates, expert_ids.astype(F32)], axis=1),...  13.5 us
    convert_element_type x1, other arithmetic, swiglu_grads(): return (jnp.where(first, gate_grad, up_grad).astype(BF16), route_part)  13.1 us
    dot_general x11, matrix products, mm(): jnp.einsum(spec, a.astype(BF16), b.astype(BF16), preferred_element_type=F32)  12.7 us
  transfers between devices with their start and end apart: 6, of which 3 were waited for; matrix products, arithmetic and copies ran while one was open for 30% of the time, Pallas kernels for 0%

commit v1 on v0

--- a/solution.py
+++ b/solution.py
@@ -1,7 +1,11 @@
+import functools
+
 import jax
 import jax.numpy as jnp
 from jax import lax
 from jax.sharding import PartitionSpec as P
+from jax.experimental import pallas as pl
+from jax.experimental.pallas import tpu as pltpu
 
 TOPK = 2
 HDIM = 64
@@ -111,18 +115,461 @@
     return (x_grad, b_grad.reshape(length, state), c_grad.reshape(length, state), step_grads)
 
 
-def swiglu_grads(upstream, gate_values, saved_rows):
-    gate_pre = saved_rows[:, 0:1, :].astype(F32)
-    up_pre = saved_rows[:, 1:2, :].astype(F32)
-    sigmoid_gate = jax.nn.sigmoid(gate_pre)
-    activated = gate_pre * sigmoid_gate
-    up = upstream[:, None, :]
-    route_part = jnp.sum(activated * up_pre * up, axis=(1, 2))
-    hidden_grad = gate_values[:, None, None] * up
-    gate_grad = hidden_grad * up_pre * sigmoid_gate * (1.0 + gate_pre * (1.0 - sigmoid_gate))
-    up_grad = hidden_grad * activated
-    first = lax.broadcasted_iota(jnp.int32, saved_rows.shape, 1) == 0
-    return (jnp.where(first, gate_grad, up_grad).astype(BF16), route_part)
+MESH_IDS = pl.DeviceIdType.MESH
+TRANSPOSED = (((1,), (1,)), ((), ()))
+
+
+def col_tile(width):
+    return 256 if width % 256 == 0 else 128
+
+
+def expert_kernel(
+    parts,
+    groups,
+    x_grad,
+    entries,
+    weight_in,
+    outgoing,
+    down_in,
+    saved_in,
+    out,
+    totals_out,
+    table,
+    gates,
+    picked,
+    rows_all,
+    weight,
+    residual,
+    down,
+    moe,
+    upstream,
+    saved,
+    staged,
+    partial,
+    route,
+    route_in,
+    totals,
+    local_sem,
+    saved_sem,
+    staged_sem,
+    send_sem,
+    recv_sem,
+    table_send,
+    table_recv,
+    pick_send,
+    pick_recv,
+    residual_send,
+    residual_recv,
+    route_sem,
+):
+    slots, columns = picked.shape[1:]
+    capacity = slots // groups
+    tokens = entries.shape[1]
+    devices = parts * groups
+    depth = weight.shape[0]
+    hidden = down.shape[0]
+    half = slots // 2
+    me = lax.axis_index("seq")
+    expert = lax.axis_index("exp")
+    square = parts == 4
+    peers = [lax.rem(me + o, parts) for o in range(1, parts)]
+    beside = me + 1 - 2 * lax.rem(me, 2)
+    across = lax.rem(me + 2, parts)
+    corner = parts - 1 - me
+
+    def local(source, target, number):
+        return pltpu.make_async_copy(source, target, local_sem.at[number])
+
+    weights_in = [
+        local(weight_in.at[j], weight.at[:, pl.ds(j * columns, columns)], j)
+        for j in range(groups)
+    ]
+    down_copy = local(down_in.at[0], down, groups)
+    flat = me * groups + expert
+    my_columns = pl.ds(pl.multiple_of(expert * columns, columns), columns)
+    my_block = pl.ds(pl.multiple_of(flat * capacity, capacity), capacity)
+
+    def outgoing_block(part, number):
+        return outgoing.at[
+            pl.ds(pl.multiple_of(number * capacity, capacity), capacity),
+            pl.ds(pl.multiple_of(part * depth, depth), depth),
+        ]
+
+    own_entries = pltpu.make_async_copy(entries, table.at[flat], table_recv)
+    own_rows = pltpu.make_async_copy(picked.at[expert], rows_all.at[me, :, my_columns], pick_recv)
+    own_residual = pltpu.make_async_copy(
+        outgoing_block(me, expert), residual.at[my_block], residual_recv.at[me]
+    )
+
+    def saved_copy(k):
+        return pltpu.make_async_copy(
+            saved_in.at[0, pl.ds(k * slots, slots)], saved.at[k % 2], saved_sem.at[k % 2]
+        )
+
+    def staged_copy(k):
+        return pltpu.make_async_copy(
+            staged.at[k % 2], out.at[0, pl.ds(k * slots, slots)], staged_sem.at[k % 2]
+        )
+
+    own_entries.start()
+    own_residual.start()
+    for copy in weights_in:
+        copy.start()
+    saved_copy(0).start()
+    down_copy.start()
+
+    barrier = pltpu.get_barrier_semaphore()
+
+    def device(other):
+        return (lax.div(other, groups), lax.rem(other, groups))
+
+    def greet(o, carry):
+        other = lax.rem(flat + o, devices)
+        pl.semaphore_signal(barrier, inc=1, device_id=device(other), device_id_type=MESH_IDS)
+        return carry
+
+    lax.fori_loop(1, devices, greet, 0)
+    pl.semaphore_wait(barrier, devices - 1)
+
+    def pick_copy(o):
+        other = lax.rem(expert + o, groups)
+        return pltpu.make_async_remote_copy(
+            src_ref=picked.at[other],
+            dst_ref=rows_all.at[me, :, my_columns],
+            send_sem=pick_send,
+            recv_sem=pick_recv,
+            device_id=(me, other),
+            device_id_type=MESH_IDS,
+        )
+
+    def residual_copy(o):
+        other = lax.rem(flat + o, devices)
+        return pltpu.make_async_remote_copy(
+            src_ref=outgoing_block(*device(other)),
+            dst_ref=residual.at[my_block],
+            send_sem=residual_send,
+            recv_sem=residual_recv.at[me],
+            device_id=device(other),
+            device_id_type=MESH_IDS,
+        )
+
+    def start_pick(o, carry):
+        pick_copy(o).start()
+        return carry
+
+    def start_residual(o, carry):
+        residual_copy(o).start()
+        return carry
+
+    def start_entries(o, carry):
+        other = lax.rem(flat + o, devices)
+        pltpu.make_async_remote_copy(
+            src_ref=entries,
+            dst_ref=table.at[flat],
+            send_sem=table_send,
+            recv_sem=table_recv,
+            device_id=device(other),
+            device_id_type=MESH_IDS,
+        ).start()
+        return carry
+
+    def pick(b, carry):
+        entry = table[me * groups + b]
+        numbers = lax.broadcasted_iota(jnp.int32, (slots, tokens), 0).astype(F32)
+        hit = jnp.zeros((slots, tokens), F32)
+        for j in range(TOPK):
+            hit = jnp.where(numbers == entry[j : j + 1], 1.0, hit)
+        block = x_grad[pl.ds(pl.multiple_of(b * tokens, tokens), tokens), :]
+        found = jnp.dot(hit.astype(BF16), block, preferred_element_type=F32).astype(BF16)
+        place = pl.ds(pl.multiple_of(b * capacity, capacity), capacity)
+        picked[:, place, :] = found.reshape(groups, capacity, columns)
+        return carry
+
+    def gate(block, carry):
+        entry = table[block]
+        numbers = lax.broadcasted_iota(jnp.int32, (capacity, tokens), 0) + expert * capacity
+        numbers = numbers.astype(F32)
+        value = jnp.zeros((capacity, tokens), F32)
+        for j in range(TOPK):
+            value = jnp.where(numbers == entry[j : j + 1], entry[TOPK + j : TOPK + j + 1], value)
+        place = pl.ds(pl.multiple_of(block * capacity, capacity), capacity)
+        gates[place, :] = jnp.sum(value, axis=1, keepdims=True)
+        return carry
+
+    def await_all(block, sem):
+        pltpu.make_async_copy(block, block, sem).wait()
+
+    def piece(phase, owner, number):
+        span = slots if number is None else half
+        first = 0 if number is None else number * half
+        if phase == 0:
+            return rows_all.at[owner, pl.ds(first, span)]
+        start = pl.multiple_of(owner * depth, depth)
+        return moe.at[phase - 1, pl.ds(first, span), pl.ds(start, depth)]
+
+    def remote(phase, owner, number, peer, index):
+        block = piece(phase, owner, number)
+        return pltpu.make_async_remote_copy(
+            src_ref=block,
+            dst_ref=block,
+            send_sem=send_sem.at[phase, index],
+            recv_sem=recv_sem.at[phase, index],
+            device_id=(peer, expert),
+            device_id_type=MESH_IDS,
+        )
+
+    def sends(phase):
+        if not square:
+            return [remote(phase, me, None, peers[o], o) for o in range(parts - 1)]
+        return [
+            remote(phase, me, 1, beside, 1),
+            remote(phase, me, 0, across, 2),
+            remote(phase, me, 0, beside, 0),
+            remote(phase, me, 1, across, 3),
+        ]
+
+    def forward_across(phase):
+        return remote(phase, beside, 1, across, 5)
+
+    def forward_beside(phase):
+        return remote(phase, across, 0, beside, 4)
+
+    def start(phase):
+        for copy in sends(phase):
+            copy.start()
+
+    def relay(phase):
+        if square:
+            remote(phase, beside, 1, beside, 1).wait_recv()
+            forward_across(phase).start()
+            remote(phase, across, 0, across, 2).wait_recv()
+            forward_beside(phase).start()
+
+    def arrive(phase):
+        if square:
+            remote(phase, beside, 0, beside, 0).wait_recv()
+            remote(phase, across, 1, across, 3).wait_recv()
+            remote(phase, corner, 0, beside, 4).wait_recv()
+            remote(phase, corner, 1, across, 5).wait_recv()
+        else:
+            for o in range(parts - 1):
+                owner = lax.rem(me + parts - 1 - o, parts)
+                remote(phase, owner, None, peers[o], o).wait_recv()
+
+    def finish(phase):
+        for copy in sends(phase):
+            copy.wait_send()
+        if square:
+            forward_across(phase).wait_send()
+            forward_beside(phase).wait_send()
+
+    def project(k):
+        tile = col_tile(depth)
+        rows = rows_all.at[k]
+        await_all(residual.at[pl.ds(k * slots, slots)], residual_recv.at[k])
+
+        def step(i, carry):
+            first = pl.multiple_of(i * tile, tile)
+            total = lax.dot_general(
+                rows[...], weight[pl.ds(first, tile), :], TRANSPOSED,
+                preferred_element_type=F32,
+            )
+            total = total + residual[pl.ds(k * slots, slots), pl.ds(first, tile)].astype(F32)
+            place = pl.multiple_of(me * depth + first, tile)
+            moe[k, :, pl.ds(place, tile)] = total.astype(BF16)
+            return carry
+
+        lax.fori_loop(0, depth // tile, step, 0)
+
+    def expand(k):
+        tile = col_tile(hidden)
+
+        def step(i, carry):
+            first = pl.multiple_of(i * tile, tile)
+            upstream[:, pl.ds(first, tile)] = lax.dot_general(
+                moe[k], down[pl.ds(first, tile), :], TRANSPOSED,
+                preferred_element_type=F32,
+            )
+            return carry
+
+        lax.fori_loop(0, hidden // tile, step, 0)
+
+    def activate(k):
+        tile = 32
+        lanes = 128
+
+        def step(i, carry):
+            first = pl.multiple_of(i * tile, tile)
+            rows = pl.ds(first, tile)
+            gate_pre = saved[k % 2, rows, 0, :].astype(F32)
+            up_pre = saved[k % 2, rows, 1, :].astype(F32)
+            up = upstream[rows, :]
+            sigmoid_gate = 1.0 / (1.0 + jnp.exp(-gate_pre))
+            activated = gate_pre * sigmoid_gate
+            product = activated * up_pre * up
+            total = product[:, :lanes]
+            for j in range(1, hidden // lanes):
+                total = total + product[:, j * lanes : (j + 1) * lanes]
+            partial[rows, :] = total
+            scale = gates[pl.ds(pl.multiple_of(k * slots + first, tile), tile), :]
+            hidden_grad = scale * up
+            gate_grad = hidden_grad * up_pre * sigmoid_gate * (1.0 + gate_pre * (1.0 - sigmoid_gate))
+            staged[k % 2, rows, 0, :] = gate_grad.astype(BF16)
+            staged[k % 2, rows, 1, :] = (hidden_grad * activated).astype(BF16)
+            return carry
+
+        lax.fori_loop(0, slots // tile, step, 0)
+        sums = jnp.sum(partial[...].T, axis=0, keepdims=True)
+        route[k] = sums
+
+        @pl.when(me == k)
+        def _():
+            route_in[k] = sums
+
+        @pl.when(me != k)
+        def _():
+            route_copy(k).start()
+
+    def route_copy(k):
+        return pltpu.make_async_remote_copy(
+            src_ref=route.at[k],
+            dst_ref=route_in.at[me],
+            send_sem=route_sem.at[0],
+            recv_sem=route_sem.at[1],
+            device_id=(k, expert),
+            device_id_type=MESH_IDS,
+        )
+
+    def total_copy(o):
+        return pltpu.make_async_remote_copy(
+            src_ref=totals.at[expert],
+            dst_ref=totals.at[expert],
+            send_sem=route_sem.at[2],
+            recv_sem=route_sem.at[3],
+            device_id=(me, lax.rem(expert + o, groups)),
+            device_id_type=MESH_IDS,
+        )
+
+    def send_totals():
+        await_all(route_in.at[pl.ds(0, parts - 1)], route_sem.at[1])
+        total = route_in[0]
+        for k in range(1, parts):
+            total = total + route_in[k]
+        totals[expert] = total
+        for o in range(1, groups):
+            total_copy(o).start()
+
+    def receive_totals():
+        await_all(totals.at[pl.ds(0, groups - 1)], route_sem.at[3])
+        totals_out[...] = totals[...]
+        await_all(route.at[pl.ds(0, parts - 1)], route_sem.at[0])
+        await_all(totals.at[pl.ds(0, groups - 1)], route_sem.at[2])
+
+    lax.fori_loop(1, devices, start_entries, 0)
+    await_all(table, table_recv)
+    lax.fori_loop(0, groups, pick, 0)
+    lax.fori_loop(0, devices, gate, 0)
+    own_rows.start()
+    lax.fori_loop(1, groups, start_pick, 0)
+    lax.fori_loop(1, devices, start_residual, 0)
+    await_all(rows_all.at[me], pick_recv)
+    start(0)
+    for copy in weights_in:
+        copy.wait()
+    relay(0)
+    arrive(0)
+    project(0)
+    start(1)
+    if parts > 1:
+        project(1)
+    relay(1)
+    start(2)
+    project(2)
+    down_copy.wait()
+    for k in range(parts):
+        arrive(k + 1)
+        if k + 1 < parts:
+            saved_copy(k + 1).start()
+        expand(k)
+        if k + 1 < parts:
+            relay(k + 2)
+            if k + 2 < parts:
+                start(k + 3)
+                if k + 3 < parts:
+                    project(k + 3)
+        saved_copy(k).wait()
+        if k >= 2:
+            staged_copy(k - 2).wait()
+        activate(k)
+        staged_copy(k).start()
+    send_totals()
+    await_all(table.at[pl.ds(0, devices - 1)], table_send)
+    await_all(picked.at[pl.ds(0, groups - 1)], pick_send)
+    await_all(residual.at[pl.ds(0, (devices - 1) * capacity)], residual_send)
+    for phase in range(parts + 1):
+        finish(phase)
+    receive_totals()
+    for k in range(max(0, parts - 2), parts):
+        staged_copy(k).wait()
+
+
+def expert_part(x_grad, entries, weight, outgoing, w_down, saved_pre):
+    groups = lax.axis_size("exp")
+    parts = lax.axis_size("seq")
+    slots = outgoing.shape[0]
+    columns = x_grad.shape[1]
+    depth = weight.shape[1]
+    hidden = w_down.shape[1]
+    width = w_down.shape[2]
+    anywhere = pl.BlockSpec(memory_space=pl.ANY)
+    in_vmem = pl.BlockSpec(memory_space=pltpu.VMEM)
+    copies = 6 if parts == 4 else parts - 1
+    return pl.pallas_call(
+        functools.partial(expert_kernel, parts, groups),
+        out_shape=(
+            jax.ShapeDtypeStruct(saved_pre.shape, BF16),
+            jax.ShapeDtypeStruct((groups, 1, slots), F32),
+        ),
+        in_specs=[in_vmem] * 2 + [anywhere] * 4,
+        out_specs=(anywhere, in_vmem),
+        scratch_shapes=[
+            pltpu.VMEM((parts * groups, *entries.shape), F32),
+            pltpu.VMEM((parts * slots, 1), F32),
+            pltpu.VMEM((groups, slots, columns), BF16),
+            pltpu.VMEM((parts, slots, groups * columns), BF16),
+            pltpu.VMEM((depth, groups * columns), BF16),
+            pltpu.VMEM((parts * slots, depth), BF16),
+            pltpu.VMEM((hidden, width), BF16),
+            pltpu.VMEM((parts, slots, width), BF16),
+            pltpu.VMEM((slots, hidden), F32),
+            pltpu.VMEM((2, slots, 2, hidden), BF16),
+            pltpu.VMEM((2, slots, 2, hidden), BF16),
+            pltpu.VMEM((slots, 128), F32),
+            pltpu.VMEM((parts, 1, slots), F32),
+            pltpu.VMEM((parts, 1, slots), F32),
+            pltpu.VMEM((groups, 1, slots), F32),
+            pltpu.SemaphoreType.DMA((groups + 1,)),
+            pltpu.SemaphoreType.DMA((2,)),
+            pltpu.SemaphoreType.DMA((2,)),
+            pltpu.SemaphoreType.DMA((parts + 1, copies)),
+            pltpu.SemaphoreType.DMA((parts + 1, copies)),
+            pltpu.SemaphoreType.DMA,
+            pltpu.SemaphoreType.DMA,
+            pltpu.SemaphoreType.DMA,
+            pltpu.SemaphoreType.DMA,
+            pltpu.SemaphoreType.DMA,
+            pltpu.SemaphoreType.DMA((parts,)),
+            pltpu.SemaphoreType.DMA((4,)),
+        ],
+        compiler_params=pltpu.CompilerParams(
+            collective_id=1, has_side_effects=True, vmem_limit_bytes=62 * 1024 * 1024
+        ),
+        cost_estimate=pl.CostEstimate(
+            flops=2 * parts * slots * (width * hidden + groups * columns * depth),
+            bytes_accessed=2 * (hidden * width + 4 * parts * slots * hidden),
+            transcendentals=0,
+        ),
+    )(x_grad, entries, weight, outgoing, w_down, saved_pre)
 
 
 def per_device(
@@ -143,85 +590,39 @@
     expert_count = lax.axis_size("exp")
     parts = lax.axis_size("seq")
     my_expert = lax.axis_index("exp")
-    my_part = lax.axis_index("seq")
     tokens_here, width = residual_grad.shape
     per_block = tokens_here * TOPK
     capacity = per_block // expert_count
     slots = expert_count * capacity
 
-    routing = lax.all_gather(
-        jnp.concatenate([gates, expert_ids.astype(F32)], axis=1), "exp", axis=0
-    )
-    part_gates = routing[:, :, :TOPK].reshape(expert_count, per_block)
-    part_ids = routing[:, :, TOPK:].astype(jnp.int32).reshape(expert_count, per_block)
+    entry_ids = expert_ids.reshape(1, per_block)
+    own_target = (entry_ids * capacity + slot_positions(entry_ids, expert_count)).reshape(
+        tokens_here, TOPK
+    )
+    slot_numbers = jnp.arange(slots, dtype=jnp.int32)
+    own_selector = jnp.any(own_target[None] == slot_numbers[:, None, None], axis=2).astype(BF16)
+    outgoing = jnp.dot(own_selector, residual_grad, preferred_element_type=F32).astype(BF16)
     slice_weight = lax.all_gather(in_weight, "exp", axis=0)
-    positions = slot_positions(part_ids, expert_count)
-    mine = (part_ids == my_expert)[:, None, :] & (
-        positions[:, None, :] == jnp.arange(capacity, dtype=jnp.int32)[None, :, None]
-    )
-    part_slot_gates = jnp.sum(jnp.where(mine, part_gates[:, None, :], 0.0), axis=2).reshape(-1)
-    slot_gates = lax.all_gather(part_slot_gates, "seq", axis=0, tiled=True)
-    part_targets = part_ids * capacity + positions
-    hits = (
-        part_targets.reshape(expert_count, 1, tokens_here, TOPK)
-        == jnp.arange(slots, dtype=jnp.int32)[None, :, None, None]
-    )
-    selector = jnp.any(hits, axis=3).astype(BF16)
-    own_selector = lax.dynamic_index_in_dim(selector, my_expert, 0, keepdims=False)
-    outgoing = jnp.dot(own_selector, residual_grad, preferred_element_type=F32).astype(BF16)
-    depth = width // parts
-    outgoing = outgoing.reshape(slots, parts, depth).transpose(1, 0, 2)
-    residual_rows = lax.all_to_all(
-        outgoing.reshape(parts * expert_count, capacity, depth), ("seq", "exp"), 0, 0, tiled=True
-    ).reshape(parts * slots, depth)
-
+    entries = jnp.concatenate([own_target.astype(F32).T, gates.T], axis=0)
+    entries = jnp.pad(entries, ((0, -entries.shape[0] % 8), (0, 0)))
     x_grad, b_grad, c_grad, step_grads = ssm_part(
         ssm_in, b_proj, c_proj, step_sizes, a_log, skip_gain, ssm_grad
     )
 
-    columns = x_grad.shape[1]
-    picked = jnp.einsum(
-        "bst,btc->bsc",
-        selector,
-        x_grad.reshape(expert_count, tokens_here, columns),
-        preferred_element_type=F32,
-    ).astype(BF16)
-    picked = picked.reshape(expert_count, expert_count, capacity, columns).transpose(1, 0, 2, 3)
-    rows = lax.all_to_all(
-        picked.reshape(expert_count, slots, columns), "exp", 0, 0, tiled=True
-    )
-    rows = rows.transpose(1, 0, 2).reshape(slots, expert_count * columns)
-    all_rows = lax.all_gather(rows, "seq", axis=0, tiled=True)
-    wide = slice_weight.transpose(1, 0, 2).reshape(depth, expert_count * columns)
-    summed = lax.dot_general(all_rows, wide, (((1,), (1,)), ((), ())), preferred_element_type=F32)
-    moe_rows = (residual_rows.astype(F32) + summed).astype(BF16)
-    gathered = lax.all_gather(moe_rows, "seq", axis=0)
-
-    both, gathered = lax.optimization_barrier(
-        (jnp.concatenate([b_grad, c_grad], axis=1), gathered)
+    both = jnp.concatenate([b_grad, c_grad], axis=1)
+    both, slice_weight = lax.optimization_barrier((both, slice_weight))
+    pre_grad, totals = expert_part(
+        x_grad, entries, slice_weight, outgoing, w_down, saved_pre
     )
     both = lax.psum_scatter(both, "exp", scatter_dimension=0, tiled=True)
     state = b_proj.shape[1]
 
-    upstream = sum(
-        lax.dot_general(
-            gathered[i],
-            w_down[0][:, i * depth : (i + 1) * depth],
-            (((1,), (1,)), ((), ())),
-            preferred_element_type=F32,
-        )
-        for i in range(parts)
-    )
-    pre_grad, route_part = swiglu_grads(upstream, slot_gates, saved_pre[0])
-    everyone = lax.all_gather(route_part, "seq", axis=0)
-    own = lax.dynamic_slice_in_dim(everyone, my_part * slots, slots, 1)
-    own = jnp.sum(own, axis=0).reshape(expert_count, capacity)
-    totals = lax.all_to_all(own, "exp", 0, 0, tiled=True).reshape(-1)
-    own_target = lax.dynamic_index_in_dim(part_targets, my_expert, 0, keepdims=False)
-    chosen = own_target[:, None] == jnp.arange(slots, dtype=jnp.int32)[None, :]
+    totals = lax.dynamic_slice_in_dim(totals[:, 0, :], my_expert * capacity, capacity, 1)
+    totals = totals.reshape(-1)
+    chosen = own_target.reshape(per_block, 1) == slot_numbers[None, :]
     route_grads = jnp.sum(jnp.where(chosen, totals[None, :], 0.0), axis=1)
     return (
-        pre_grad[None],
+        pre_grad,
         route_grads.reshape(tokens_here, TOPK),
         both[:, :state],
         both[:, state:],

time: 345 us -> 265 us (0.77)
  Pallas kernels: 0 us -> 185 us
  waiting for transfers between devices: 110 us -> 11.5 us
  blocking collectives: 66.5 us -> 8.28 us
  matrix products: 65.4 us -> 14.4 us
  other arithmetic: 36.8 us -> 6.96 us
  local copies, waits for them, and re-layouts: 36.5 us -> 23.2 us
  starting transfers between devices: 12.7 us -> 0.08 us
    pallas_call x0 -> x1, Pallas kernels: none -> 185 us  [expert_part(): pl.pallas_call(functools.partial(expert_kernel, parts, groups), out_shape...]
    all_gather x2 -> x0, waiting for transfers between devices: 67.2 us -> none  [the longest x1 50.7 us: per_device(): gathered = lax.all_gather(moe_rows, 'seq', axis=0)]
    dot_general x6 -> x0, matrix products: 50.2 us -> none  [the longest x4 38.6 us: per_device(): lax.dot_general(gathered[i], w_down[0][:, i * depth:(i + 1) * depth], (((...]
    all_to_all x2 -> x0, waiting for transfers between devices: 41.7 us -> none  [the longest x1 41.7 us: per_device(): lax.all_to_all(outgoing.reshape(parts * expert_count, capacity, depth), (...]
    all_to_all x1 -> x0, blocking collectives: 30.4 us -> none  [per_device(): lax.all_to_all(picked.reshape(expert_count, slots, columns), 'exp', 0, 0,...]
    all_gather x3 -> x0, blocking collectives: 27.5 us -> none  [the longest x1 13.5 us: per_device(): lax.all_gather(jnp.concatenate([gates, expert_ids.astype(F32)], axis=1),...]
    convert_element_type x2 -> x0, other arithmetic: 13.8 us -> none  [the longest x1 13.1 us: swiglu_grads(): return (jnp.where(first, gate_grad, up_grad).astype(BF16), route_part)]
    all_to_all x2 -> x0, starting transfers between devices: 12.3 us -> none  [the longest x1 7.17 us: per_device(): totals = lax.all_to_all(own, 'exp', 0, 0, tiled=True).reshape(-1)]
  transfers between devices with their start and end apart: 6 -> 2, of which waited for: 3 -> 1; matrix products, arithmetic and copies ran while one was open for 30% -> 13% of each run, Pallas kernels for 0% -> 70%
where the time goes in v1:
time: 265 us; the launch traced here: 264 us
  Pallas kernels  185 us (70%)
  local copies, waits for them, and re-layouts  23.2 us (9%)
  between operations  14.6 us (6%)
  matrix products  14.4 us (5%)
  waiting for transfers between devices  11.5 us (4%)
  blocking collectives  8.28 us (3%)
  other arithmetic  6.96 us (3%)
    pallas_call x1, Pallas kernels, expert_part(): pl.pallas_call(functools.partial(expert_kernel, parts, groups), out_shape...  185 us
    unnamed x59, local copies, waits for them, and re-layouts  11.5 us
    dot_general x11, matrix products, mm(): jnp.einsum(spec, a.astype(BF16), b.astype(BF16), preferred_element_type=F32)  11.3 us
    all_gather x1, waiting for transfers between devices, per_device(): slice_weight = lax.all_gather(in_weight, 'exp', axis=0)  10.8 us
    all_gather x1, blocking collectives, ssm_part(): everyone = lax.all_gather(packed, 'seq', axis=0).astype(F32)  8.28 us
  transfers between devices with their start and end apart: 2, of which 1 were waited for; matrix products, arithmetic and copies ran while one was open for 13% of the time, Pallas kernels for 70%

profile of v1, /device:TPU:7, one launch (start us, length us, event | category | flops | bytes accessed | tf_op | source)
XLA Modules:
  0.0 264.1 jit_solution(7534545367719702152)
XLA Ops:
  7.3 0.7 all-gather.3.cloned.1.call-update
  8.0 2.1 reshape.253
  10.1 0.5 copy.116
  10.7 1.3 copy.142
  12.0 0.6 copy-done.22
  12.6 0.1 broadcast_multiply_fusion.1
  12.7 0.3 fusion.50
  13.0 0.2 slice_reduce_fusion.1
  13.2 0.1 subtract_exponential_fusion
  13.3 0.3 copy-done.6
  13.7 0.1 copy.121
  13.8 0.1 eq.57
  13.9 0.3 fusion.31
  14.2 0.6 multiply_add_fusion.4
  14.8 0.1 sub.49
  14.9 0.7 copy.122
  15.6 1.2 copy.111
  16.8 0.4 reshape.239
  17.2 0.2 slice_reduce_fusion.3
  17.4 0.3 convolution_bitcast_fusion.3
  17.7 0.3 convolution_bitcast_fusion.4
  18.0 0.1 fusion.82
  18.2 0.1 broadcast_in_dim.67
  18.3 8.3 %all_gather.10 = bf16[4,4,144,128]{3,2,1,0:T(8,128)(2,1)S(1)} all-gather(bf16[1,4,144,128]{3,2,1,0:T(8,128)(2,1)S(1)} %pad_maximum_fusion.3), channel_id=1, replica_groups=mesh['seq'=4,'exp'=8] {'seq'}, dimensions={0}, use_global_device_ids=true | all-gather | bytes 737280 | tf_op jit(solution)/shard_map/all_gather | solution.py:68
  26.5 0.1 convert_element_type.102
  26.7 0.1 slice_bitcast_fusion
  26.8 0.1 add_bitcast_fusion.1
  26.9 0.1 fusion.87
  27.0 0.1 fusion.88
  27.1 0.1 add_bitcast_fusion
  27.2 0.6 copy-done.4
  27.8 0.7 multiply_reduce_fusion.1
  28.6 1.4 copy.130
  29.9 0.9 multiply_reduce_fusion.2
  30.9 1.3 fusion.26
  32.1 0.3 fusion.107
  32.5 3.8 %fusion.3 = (f32[4,4,256]{2,1,0:T(4,128)S(1)}, f32[4,4,256]{2,1,0:T(4,128)S(1)}, bf16[4,256,256]{2,1,0:T(8,128)(2,1)S(1)}) fusion(f32[4,256,256]{2,1,0:T(8,128)S(1)} %fusion.107, f32[4,4,256]{2,1,0:T(4,128)} %copy-done.6, pred[256,256]{1,0:T(8,128)(4,1)S(1)} %iota_compare_fusion.3, bf16[4,256,4,64]{1,3,0,2:T(8,128)(2,1)} %copy.142, ...), kind=kOutput, calls=%fused_computation.6 | convolution fusion | flops 144433152 | bytes 2736128 | tf_op jit(solution)/shard_map/hkip,hkjp->hkij/dot_general | solution.py:21
  36.3 0.2 fusion.48
  36.5 1.4 fusion.33
  37.9 0.2 fusion.29
  38.1 0.6 copy.146
  38.8 0.6 convert_bitcast_fusion
  39.3 0.6 fusion.57
  40.0 0.3 convolution_bitcast_fusion.2
  40.3 0.3 convolution_bitcast_fusion.1
  40.7 0.3 convolution_add_fusion
  41.0 0.3 convolution_add_fusion.1
  41.4 1.0 pad_maximum_fusion
  42.4 0.1 fusion.84
  42.5 2.0 convolution_convert_fusion.outgoing
  44.6 2.7 %fusion.23 = bf16[4,256,4,64]{1,3,0,2:T(8,128)(2,1)S(1)} fusion(f32[4,256,256]{2,1,0:T(8,128)} %copy-done.3, f32[4,4,256]{2,1,0:T(4,128)S(1)} %copy-done.7, pred[256,256]{1,0:T(8,128)(4,1)S(1)} %copy-done.10, f32[4,4,64,256]{3,2,1,0:T(8,128)} %get-tuple-element.69, f32[4]{0:T(128)S(1)} %copy-done.26, f32[4,256,4]{1,0,2:T(4,128)S(1)} %fusion.84, ...), kind=kOutput, calls=%fused_computation.23 | convolution fusion | flops 142082048 | bytes 3244048 | tf_op jit(solution)/shard_map/hkij,hkip->hkjp/dot_general | solution.py:21
  47.3 10.8 %all-gather.3.cloned.1.call-done = bf16[8192,256]{1,0:T(8,128)(2,1)} async-done(((bf16[1024,256]{1,0:T(8,128)(2,1)}), bf16[8192,256]{1,0:T(8,128)(2,1)}) %all-gather.3.cloned.1.call-update) | async-done | bytes 4194320 | tf_op jit(solution)/shard_map/all_gather | solution.py:605
  58.1 0.7 broadcast_multiply_fusion
  58.8 0.6 copy.140
  59.5 1.5 reshape.254.x_grad
  61.0 0.6 select_maximum_fusion.entries
  61.6 185.1 %shard_map.164 = (bf16[1,1024,2,1792]{3,2,1,0:T(2,128)(2,1)}, f32[8,1,256]{2,1,0:T(1,128)}) custom-call(bf16[1024,256]{1,0:T(8,128)(2,1)} %reshape.254.x_grad, f32[8,128]{1,0:T(8,128)} %select_maximum_fusion.entries, bf16[8,1024,256]{2,1,0:T(8,128)(2,1)} %bitcast.250, bf16[256,4096]{1,0:T(8,128)(2,1)} %convolution_convert_fusion.outgoing, ...), custom_call_target="tpu_custom_call" | custom-call | flops 19327352832 | bytes 29360128 | tf_op jit(solution)/shard_map/pallas_call | solution.py:527
  246.7 0.8 dynamic-slice_reduce_fusion
  247.4 0.1 broadcast_in_dim.70
  247.5 0.2 select_reduce_fusion
  247.7 0.1 reshape.243
  247.9 0.6 copy.131
  248.5 1.5 fusion.106
  250.0 7.3 %copy.167 = bf16[1,1024,2,1792]{3,2,1,0:T(2,128)(2,1)} copy(bf16[1,1024,2,1792]{3,2,1,0:T(2,128)(2,1)} %get-tuple-element.77) | data formatting | bytes 14680064
  (67 shorter events, 0.3 us)
Async XLA Ops:
  7.2 35.4 %copy-start = (bf16[128,4096]{1,0:T(8,128)(2,1)S(1)}, bf16[128,4096]{1,0:T(8,128)(2,1)}, u32[]{:S(2)}) copy-start(bf16[128,4096]{1,0:T(8,128)(2,1)} %param.17) | copy-start | bytes 3145732
  7.2 4.8 %copy-start.25 = (f32[4]{0:T(128)S(1)}, f32[4]{0:T(128)}, u32[]{:S(2)}) copy-start(f32[4]{0:T(128)} %param.23) | copy-start | bytes 52
  7.2 5.4 %copy-start.16 = (f32[4,1024]{1,0:T(4,128)S(1)}, f32[4,1024]{1,0:T(4,128)}, u32[]{:S(2)}) copy-start(f32[4,1024]{1,0:T(4,128)} %param.22) | copy-start | bytes 49156
  7.2 6.4 %copy-start.17 = (s32[128,2]{0,1:T(2,128)S(1)}, s32[128,2]{0,1:T(2,128)}, u32[]{:S(2)}) copy-start(s32[128,2]{0,1:T(2,128)} %param.14) | copy-start | bytes 3076
  7.2 10.2 %copy-start.2 = (bf16[1024,128]{1,0:T(8,128)(2,1)S(1)}, bf16[1024,128]{1,0:T(8,128)(2,1)}, u32[]{:S(2)}) copy-start(bf16[1024,128]{1,0:T(8,128)(2,1)} %param.21) | copy-start | bytes 786436
  7.2 50.9 %all-gather.3.cloned.1.call-start = ((), (), s32[]{:S(2)}) async-start(), calls=%async_computation.2 | async-start | bytes 4718592 | tf_op jit(solution)/shard_map/all_gather | solution.py:605
  8.0 240.5 %reduce-scatter.2.cloned.1.call-start = ((), (), s32[]{:S(2)}) async-start(), calls=%async_computation.1 | async-start | bytes 1179648 | tf_op jit(solution)/shard_map/reduce_scatter | solution.py:617
  8.0 9.7 %copy-start.1 = (bf16[1024,128]{1,0:T(8,128)(2,1)S(1)}, bf16[1024,128]{1,0:T(8,128)(2,1)}, u32[]{:S(2)}) copy-start(bf16[1024,128]{1,0:T(8,128)(2,1)} %param.20) | copy-start | bytes 786436
  12.0 0.6 copy-start.22
  13.0 0.6 copy-start.6
  13.2 13.4 %copy-start.14 = (f32[4,4]{1,0:T(4,128)}, f32[4,4]{1,0:T(4,128)S(1)}, u32[]{:S(2)}) copy-start(f32[4,4]{1,0:T(4,128)S(1)} %get-tuple-element.41) | copy-start | bytes 196
  13.6 13.0 %copy-start.12 = (f32[4,4,256]{2,0,1:T(4,128)}, f32[4,4,256]{2,0,1:T(4,128)S(1)}, u32[]{:S(2)}) copy-start(f32[4,4,256]{2,0,1:T(4,128)S(1)} %copy.117) | copy-start | bytes 49156
  27.2 0.7 copy-start.4
  30.8 5.4 %copy-start.9 = (pred[256,256]{1,0:T(8,128)(4,1)}, pred[256,256]{1,0:T(8,128)(4,1)S(1)}, u32[]{:S(2)}) copy-start(pred[256,256]{1,0:T(8,128)(4,1)S(1)} %iota_compare_fusion.3) | copy-start | bytes 196612
  32.4 3.8 %copy-start.3 = (f32[4,256,256]{2,1,0:T(8,128)}, f32[4,256,256]{2,1,0:T(8,128)S(1)}, u32[]{:S(2)}) copy-start(f32[4,256,256]{2,1,0:T(8,128)S(1)} %fusion.107) | copy-start | bytes 3145732
  32.5 6.3 %copy-start.18 = (s32[128,2]{0,1:T(2,128)S(1)}, s32[128,2]{0,1:T(2,128)}, u32[]{:S(2)}) copy-start(s32[128,2]{0,1:T(2,128)} %param.14) | copy-start | bytes 3076
  32.5 6.3 %copy-start.19 = (s32[128,2]{0,1:T(2,128)S(1)}, s32[128,2]{0,1:T(2,128)}, u32[]{:S(2)}) copy-start(s32[128,2]{0,1:T(2,128)} %copy.122) | copy-start | bytes 3076
  36.3 4.0 %copy-start.5 = (f32[4,64,128]{2,1,0:T(8,128)S(1)}, f32[4,64,128]{2,1,0:T(8,128)}, u32[]{:S(2)}) copy-start(f32[4,64,128]{2,1,0:T(8,128)} %copy-done.4) | copy-start | bytes 393220
  36.3 4.0 %copy-start.13 = (f32[4,4,256]{2,0,1:T(4,128)S(1)}, f32[4,4,256]{2,0,1:T(4,128)}, u32[]{:S(2)}) copy-start(f32[4,4,256]{2,0,1:T(4,128)} %copy-done.12) | copy-start | bytes 49156
  40.3 2.1 copy-start.7
  40.7 1.7 copy-start.15
  40.7 1.8 copy-start.8
  40.7 3.8 %copy-start.10 = (pred[256,256]{1,0:T(8,128)(4,1)S(1)}, pred[256,256]{1,0:T(8,128)(4,1)}, u32[]{:S(2)}) copy-start(pred[256,256]{1,0:T(8,128)(4,1)} %copy-done.9) | copy-start | bytes 196612
  40.7 3.8 %copy-start.26 = (f32[4]{0:T(128)S(1)}, f32[4]{0:T(128)}, u32[]{:S(2)}) copy-start(f32[4]{0:T(128)} %param.24) | copy-start | bytes 52
  44.6 13.6 %copy-start.11 = (f32[1,4,4,256]{3,1,2,0:T(4,128)S(1)}, f32[1,4,4,256]{3,1,2,0:T(4,128)}, u32[]{:S(2)}) copy-start(f32[1,4,4,256]{3,1,2,0:T(4,128)} %copy.146) | copy-start | bytes 49156
  44.6 13.6 %copy-start.23 = (f32[4]{0:T(128)S(1)}, f32[4]{0:T(128)}, u32[]{:S(2)}) copy-start(f32[4]{0:T(128)} %copy-done.22) | copy-start | bytes 52
  47.3 13.7 %copy-start.21 = (f32[2,128]{1,0:T(2,128)S(1)}, f32[2,128]{1,0:T(2,128)}, u32[]{:S(2)}) copy-start(f32[2,128]{1,0:T(2,128)} %get-tuple-element.51) | copy-start | bytes 3076
  47.3 13.7 %copy-start.24 = (f32[128,2]{0,1:T(2,128)S(1)}, f32[128,2]{0,1:T(2,128)}, u32[]{:S(2)}) copy-start(f32[128,2]{0,1:T(2,128)} %param.13) | copy-start | bytes 3076
  61.6 186.0 %copy-start.20 = (s32[256]{0:T(256)S(1)}, s32[256]{0:T(256)}, u32[]{:S(2)}) copy-start(s32[256]{0:T(256)} %get-tuple-element.64) | copy-start | bytes 3076
Sparse Core Ops, SparseCore 0:
  9.6 48.4 all-gather.2
  60.4 37.1 reduce-scatter.1

commit v2 on v1

--- a/solution.py
+++ b/solution.py
@@ -466,12 +466,14 @@
         await_all(totals.at[pl.ds(0, groups - 1)], route_sem.at[2])
 
     lax.fori_loop(1, devices, start_entries, 0)
+    first_batch = 1 + devices // 6
+    lax.fori_loop(1, first_batch, start_residual, 0)
     await_all(table, table_recv)
-    lax.fori_loop(0, groups, pick, 0)
-    lax.fori_loop(0, devices, gate, 0)
+    lax.fori_loop(0, groups, pick, 0, unroll=True)
     own_rows.start()
     lax.fori_loop(1, groups, start_pick, 0)
-    lax.fori_loop(1, devices, start_residual, 0)
+    lax.fori_loop(first_batch, devices, start_residual, 0)
+    lax.fori_loop(0, devices, gate, 0)
     await_all(rows_all.at[me], pick_recv)
     start(0)
     for copy in weights_in:

time: 265 us -> 270 us (1.019)
  Pallas kernels: 185 us -> 191 us
    pallas_call x1, Pallas kernels: 185 us -> 191 us  [expert_part(): pl.pallas_call(functools.partial(expert_kernel, parts, groups), out_shape...]
  transfers between devices with their start and end apart: 2 -> 2, of which waited for: 1 -> 1; matrix products, arithmetic and copies ran while one was open for 13% -> 13% of each run, Pallas kernels for 70% -> 71%
where the time goes in v2:
time: 270 us
  Pallas kernels  191 us (71%)
  local copies, waits for them, and re-layouts  23.2 us (9%)
  between operations  14.6 us (5%)
  matrix products  14.4 us (5%)
  waiting for transfers between devices  11.5 us (4%)
  blocking collectives  8.28 us (3%)
  other arithmetic  6.96 us (3%)
    pallas_call x1, Pallas kernels, expert_part(): pl.pallas_call(functools.partial(expert_kernel, parts, groups), out_shape...  191 us
    unnamed x59, local copies, waits for them, and re-layouts  11.5 us
    dot_general x11, matrix products, mm(): jnp.einsum(spec, a.astype(BF16), b.astype(BF16), preferred_element_type=F32)  11.3 us
    all_gather x1, waiting for transfers between devices, per_device(): slice_weight = lax.all_gather(in_weight, 'exp', axis=0)  10.8 us
    all_gather x1, blocking collectives, ssm_part(): everyone = lax.all_gather(packed, 'seq', axis=0).astype(F32)  8.28 us
  transfers between devices with their start and end apart: 2, of which 1 were waited for; matrix products, arithmetic and copies ran while one was open for 13% of the time, Pallas kernels for 71%

profile of v2, /device:TPU:7, one launch (start us, length us, event | category | flops | bytes accessed | tf_op | source)
XLA Modules:
  0.0 269.6 jit_solution(1852487897485546000)
XLA Ops:
  7.3 0.7 all-gather.3.cloned.1.call-update
  8.0 2.1 reshape.253
  10.1 0.5 copy.116
  10.7 1.3 copy.142
  12.0 0.6 copy-done.22
  12.6 0.1 broadcast_multiply_fusion.1
  12.7 0.3 fusion.50
  13.0 0.2 slice_reduce_fusion.1
  13.2 0.1 subtract_exponential_fusion
  13.3 0.3 copy-done.6
  13.7 0.1 copy.121
  13.8 0.1 eq.57
  13.9 0.3 fusion.31
  14.2 0.6 multiply_add_fusion.4
  14.8 0.1 sub.49
  14.9 0.7 copy.122
  15.6 1.2 copy.111
  16.8 0.4 reshape.239
  17.2 0.2 slice_reduce_fusion.3
  17.4 0.3 convolution_bitcast_fusion.3
  17.7 0.3 convolution_bitcast_fusion.4
  18.0 0.1 fusion.82
  18.2 0.1 broadcast_in_dim.67
  18.3 8.3 %all_gather.10 = bf16[4,4,144,128]{3,2,1,0:T(8,128)(2,1)S(1)} all-gather(bf16[1,4,144,128]{3,2,1,0:T(8,128)(2,1)S(1)} %pad_maximum_fusion.3), channel_id=1, replica_groups=mesh['seq'=4,'exp'=8] {'seq'}, dimensions={0}, use_global_device_ids=true | all-gather | bytes 737280 | tf_op jit(solution)/shard_map/all_gather | solution.py:68
  26.5 0.1 convert_element_type.102
  26.7 0.1 slice_bitcast_fusion
  26.8 0.1 add_bitcast_fusion.1
  26.9 0.1 fusion.87
  27.0 0.1 fusion.88
  27.1 0.1 add_bitcast_fusion
  27.2 0.6 copy-done.4
  27.8 0.7 multiply_reduce_fusion.1
  28.6 1.4 copy.130
  29.9 0.9 multiply_reduce_fusion.2
  30.9 1.3 fusion.26
  32.1 0.3 fusion.107
  32.5 3.8 %fusion.3 = (f32[4,4,256]{2,1,0:T(4,128)S(1)}, f32[4,4,256]{2,1,0:T(4,128)S(1)}, bf16[4,256,256]{2,1,0:T(8,128)(2,1)S(1)}) fusion(f32[4,256,256]{2,1,0:T(8,128)S(1)} %fusion.107, f32[4,4,256]{2,1,0:T(4,128)} %copy-done.6, pred[256,256]{1,0:T(8,128)(4,1)S(1)} %iota_compare_fusion.3, bf16[4,256,4,64]{1,3,0,2:T(8,128)(2,1)} %copy.142, ...), kind=kOutput, calls=%fused_computation.6 | convolution fusion | flops 144433152 | bytes 2736128 | tf_op jit(solution)/shard_map/hkip,hkjp->hkij/dot_general | solution.py:21
  36.3 0.2 fusion.48
  36.5 1.4 fusion.33
  37.9 0.2 fusion.29
  38.1 0.6 copy.146
  38.8 0.6 convert_bitcast_fusion
  39.3 0.6 fusion.57
  40.0 0.3 convolution_bitcast_fusion.2
  40.3 0.3 convolution_bitcast_fusion.1
  40.7 0.3 convolution_add_fusion
  41.0 0.3 convolution_add_fusion.1
  41.4 1.0 pad_maximum_fusion
  42.4 0.1 fusion.84
  42.5 2.0 convolution_convert_fusion.outgoing
  44.6 2.7 %fusion.23 = bf16[4,256,4,64]{1,3,0,2:T(8,128)(2,1)S(1)} fusion(f32[4,256,256]{2,1,0:T(8,128)} %copy-done.3, f32[4,4,256]{2,1,0:T(4,128)S(1)} %copy-done.7, pred[256,256]{1,0:T(8,128)(4,1)S(1)} %copy-done.10, f32[4,4,64,256]{3,2,1,0:T(8,128)} %get-tuple-element.69, f32[4]{0:T(128)S(1)} %copy-done.26, f32[4,256,4]{1,0,2:T(4,128)S(1)} %fusion.84, ...), kind=kOutput, calls=%fused_computation.23 | convolution fusion | flops 142082048 | bytes 3244048 | tf_op jit(solution)/shard_map/hkij,hkip->hkjp/dot_general | solution.py:21
  47.3 10.8 %all-gather.3.cloned.1.call-done = bf16[8192,256]{1,0:T(8,128)(2,1)} async-done(((bf16[1024,256]{1,0:T(8,128)(2,1)}), bf16[8192,256]{1,0:T(8,128)(2,1)}) %all-gather.3.cloned.1.call-update) | async-done | bytes 4194320 | tf_op jit(solution)/shard_map/all_gather | solution.py:607
  58.1 0.7 broadcast_multiply_fusion
  58.8 0.6 copy.140
  59.5 1.5 reshape.254.x_grad
  61.0 0.6 select_maximum_fusion.entries
  61.6 190.5 %shard_map.164 = (bf16[1,1024,2,1792]{3,2,1,0:T(2,128)(2,1)}, f32[8,1,256]{2,1,0:T(1,128)}) custom-call(bf16[1024,256]{1,0:T(8,128)(2,1)} %reshape.254.x_grad, f32[8,128]{1,0:T(8,128)} %select_maximum_fusion.entries, bf16[8,1024,256]{2,1,0:T(8,128)(2,1)} %bitcast.250, bf16[256,4096]{1,0:T(8,128)(2,1)} %convolution_convert_fusion.outgoing, ...), custom_call_target="tpu_custom_call" | custom-call | flops 19327352832 | bytes 29360128 | tf_op jit(solution)/shard_map/pallas_call | solution.py:529
  252.1 0.8 dynamic-slice_reduce_fusion
  252.9 0.1 broadcast_in_dim.70
  253.0 0.2 select_reduce_fusion
  253.1 0.1 reshape.243
  253.3 0.6 copy.131
  253.9 1.5 fusion.106
  255.5 7.3 %copy.167 = bf16[1,1024,2,1792]{3,2,1,0:T(2,128)(2,1)} copy(bf16[1,1024,2,1792]{3,2,1,0:T(2,128)(2,1)} %get-tuple-element.77) | data formatting | bytes 14680064
  (67 shorter events, 0.3 us)
Async XLA Ops:
  7.2 35.4 %copy-start = (bf16[128,4096]{1,0:T(8,128)(2,1)S(1)}, bf16[128,4096]{1,0:T(8,128)(2,1)}, u32[]{:S(2)}) copy-start(bf16[128,4096]{1,0:T(8,128)(2,1)} %param.17) | copy-start | bytes 3145732
  7.2 4.8 %copy-start.25 = (f32[4]{0:T(128)S(1)}, f32[4]{0:T(128)}, u32[]{:S(2)}) copy-start(f32[4]{0:T(128)} %param.23) | copy-start | bytes 52
  7.2 5.4 %copy-start.16 = (f32[4,1024]{1,0:T(4,128)S(1)}, f32[4,1024]{1,0:T(4,128)}, u32[]{:S(2)}) copy-start(f32[4,1024]{1,0:T(4,128)} %param.22) | copy-start | bytes 49156
  7.2 6.4 %copy-start.17 = (s32[128,2]{0,1:T(2,128)S(1)}, s32[128,2]{0,1:T(2,128)}, u32[]{:S(2)}) copy-start(s32[128,2]{0,1:T(2,128)} %param.14) | copy-start | bytes 3076
  7.2 10.2 %copy-start.2 = (bf16[1024,128]{1,0:T(8,128)(2,1)S(1)}, bf16[1024,128]{1,0:T(8,128)(2,1)}, u32[]{:S(2)}) copy-start(bf16[1024,128]{1,0:T(8,128)(2,1)} %param.21) | copy-start | bytes 786436
  7.2 50.9 %all-gather.3.cloned.1.call-start = ((), (), s32[]{:S(2)}) async-start(), calls=%async_computation.2 | async-start | bytes 4718592 | tf_op jit(solution)/shard_map/all_gather | solution.py:607
  8.0 246.0 %reduce-scatter.2.cloned.1.call-start = ((), (), s32[]{:S(2)}) async-start(), calls=%async_computation.1 | async-start | bytes 1179648 | tf_op jit(solution)/shard_map/reduce_scatter | solution.py:619
  8.0 9.7 %copy-start.1 = (bf16[1024,128]{1,0:T(8,128)(2,1)S(1)}, bf16[1024,128]{1,0:T(8,128)(2,1)}, u32[]{:S(2)}) copy-start(bf16[1024,128]{1,0:T(8,128)(2,1)} %param.20) | copy-start | bytes 786436
  12.0 0.6 copy-start.22
  13.0 0.6 copy-start.6
  13.2 13.4 %copy-start.14 = (f32[4,4]{1,0:T(4,128)}, f32[4,4]{1,0:T(4,128)S(1)}, u32[]{:S(2)}) copy-start(f32[4,4]{1,0:T(4,128)S(1)} %get-tuple-element.41) | copy-start | bytes 196
  13.6 13.0 %copy-start.12 = (f32[4,4,256]{2,0,1:T(4,128)}, f32[4,4,256]{2,0,1:T(4,128)S(1)}, u32[]{:S(2)}) copy-start(f32[4,4,256]{2,0,1:T(4,128)S(1)} %copy.117) | copy-start | bytes 49156
  27.2 0.7 copy-start.4
  30.8 5.4 %copy-start.9 = (pred[256,256]{1,0:T(8,128)(4,1)}, pred[256,256]{1,0:T(8,128)(4,1)S(1)}, u32[]{:S(2)}) copy-start(pred[256,256]{1,0:T(8,128)(4,1)S(1)} %iota_compare_fusion.3) | copy-start | bytes 196612
  32.4 3.8 %copy-start.3 = (f32[4,256,256]{2,1,0:T(8,128)}, f32[4,256,256]{2,1,0:T(8,128)S(1)}, u32[]{:S(2)}) copy-start(f32[4,256,256]{2,1,0:T(8,128)S(1)} %fusion.107) | copy-start | bytes 3145732
  32.5 6.3 %copy-start.18 = (s32[128,2]{0,1:T(2,128)S(1)}, s32[128,2]{0,1:T(2,128)}, u32[]{:S(2)}) copy-start(s32[128,2]{0,1:T(2,128)} %param.14) | copy-start | bytes 3076
  32.5 6.3 %copy-start.19 = (s32[128,2]{0,1:T(2,128)S(1)}, s32[128,2]{0,1:T(2,128)}, u32[]{:S(2)}) copy-start(s32[128,2]{0,1:T(2,128)} %copy.122) | copy-start | bytes 3076
  36.3 4.0 %copy-start.5 = (f32[4,64,128]{2,1,0:T(8,128)S(1)}, f32[4,64,128]{2,1,0:T(8,128)}, u32[]{:S(2)}) copy-start(f32[4,64,128]{2,1,0:T(8,128)} %copy-done.4) | copy-start | bytes 393220
  36.3 4.0 %copy-start.13 = (f32[4,4,256]{2,0,1:T(4,128)S(1)}, f32[4,4,256]{2,0,1:T(4,128)}, u32[]{:S(2)}) copy-start(f32[4,4,256]{2,0,1:T(4,128)} %copy-done.12) | copy-start | bytes 49156
  40.3 2.1 copy-start.7
  40.7 1.7 copy-start.15
  40.7 1.8 copy-start.8
  40.7 3.8 %copy-start.10 = (pred[256,256]{1,0:T(8,128)(4,1)S(1)}, pred[256,256]{1,0:T(8,128)(4,1)}, u32[]{:S(2)}) copy-start(pred[256,256]{1,0:T(8,128)(4,1)} %copy-done.9) | copy-start | bytes 196612
  40.7 3.8 %copy-start.26 = (f32[4]{0:T(128)S(1)}, f32[4]{0:T(128)}, u32[]{:S(2)}) copy-start(f32[4]{0:T(128)} %param.24) | copy-start | bytes 52
  44.6 13.6 %copy-start.11 = (f32[1,4,4,256]{3,1,2,0:T(4,128)S(1)}, f32[1,4,4,256]{3,1,2,0:T(4,128)}, u32[]{:S(2)}) copy-start(f32[1,4,4,256]{3,1,2,0:T(4,128)} %copy.146) | copy-start | bytes 49156
  44.6 13.6 %copy-start.23 = (f32[4]{0:T(128)S(1)}, f32[4]{0:T(128)}, u32[]{:S(2)}) copy-start(f32[4]{0:T(128)} %copy-done.22) | copy-start | bytes 52
  47.3 13.7 %copy-start.21 = (f32[2,128]{1,0:T(2,128)S(1)}, f32[2,128]{1,0:T(2,128)}, u32[]{:S(2)}) copy-start(f32[2,128]{1,0:T(2,128)} %get-tuple-element.51) | copy-start | bytes 3076
  47.3 13.7 %copy-start.24 = (f32[128,2]{0,1:T(2,128)S(1)}, f32[128,2]{0,1:T(2,128)}, u32[]{:S(2)}) copy-start(f32[128,2]{0,1:T(2,128)} %param.13) | copy-start | bytes 3076
  61.6 191.4 %copy-start.20 = (s32[256]{0:T(256)S(1)}, s32[256]{0:T(256)}, u32[]{:S(2)}) copy-start(s32[256]{0:T(256)} %get-tuple-element.64) | copy-start | bytes 3076
Sparse Core Ops, SparseCore 0:
  9.6 48.4 all-gather.2
  60.4 57.1 reduce-scatter.1
